TPU v7x, 128 devices: a whole 4x4x4 slice. The times are simulated.
128 devices in a mesh: dev: 128 (over y, z, x, core).
Axes of the slice: x: 4, y: 4, z: 4, core: 2. Of those that a mesh axis runs over, the one named last changes fastest.
Arguments:
- state_real: float32 [16777216], P('dev'), may hold values from -24 to 24, as said below
- state_imag: float32 [16777216], P('dev'), may hold values from -24 to 24, as said below
- subsystem: int32 [3], replicated, may hold values from 0 to 16, as said below
Outputs:
- rho_real: float32 [1024, 1024], P('dev')
- rho_imag: float32 [1024, 1024], P('dev')
Inputs may be any that keep to these rules, and one draw needn't show every extreme that they name: `subsystem`: the 3 entries are distinct local bit positions in ascending order; the first is always 0 and the last always 17 - 1. `state_real`: real parts of amplitudes; their typical size changes between aligned blocks of 2**(11) local indices by up to a factor of 16. `state_imag`: imaginary parts of amplitudes, with the same block sizes as the real parts.
All inputs are finite; a program needn't handle non-finite values.
Results may differ from a plain program's by a relative error of at most 0.0001.
Values sent between devices are 32-bit elements; how exact they have to be, the bound alone decides.
No kernel may reach another device: no remote copies, remote signals or barrier semaphores. Data moves between devices by JAX's collectives and lax.ppermute only.
A program may use at most 192 MiB of HBM per device.

v0:
```python
import jax
import jax.numpy as jnp
from jax import lax
from jax.sharding import Mesh
from jax.sharding import PartitionSpec as P

DEV = ("dev_0", "dev_1", "dev_2", "dev_3")


def in_blocks(value, dim, devices):
    before, after = (value.shape[:dim], value.shape[dim + 1 :])
    return jnp.moveaxis(value.reshape(*before, devices, -1, *after), dim, 0)


def sum_by_chip(value, chips, core, dim):
    sizes = (lax.axis_size(chips), lax.axis_size(core))
    blocks = in_blocks(value, dim, sizes[0] * sizes[1])
    inside = blocks.shape[1:]
    blocks = blocks.reshape(*sizes, *inside).swapaxes(0, 1).reshape(-1, *inside)
    blocks = lax.psum_scatter(blocks, core, scatter_dimension=0, tiled=True)
    return lax.psum_scatter(blocks, chips, scatter_dimension=0, tiled=True)[0]


def regroup(local_bits):
    branches = []
    for lower_count in range(local_bits - 2):

        def make_branch(flat, lower_count=lower_count):
            upper = 2 ** (local_bits - 3 - lower_count)
            lower = 2**lower_count
            shaped = flat.reshape(2, upper, 2, lower, 2)
            moved = jnp.transpose(shaped, (0, 2, 4, 1, 3))
            return moved.reshape(8, upper * lower)

        branches.append(make_branch)
    return branches


def contract(left, right):
    return lax.dot_general(
        left,
        right,
        (((1,), (1,)), ((), ())),
        precision=lax.Precision.HIGHEST,
        preferred_element_type=jnp.float32,
    )


def gram(left_re, left_im, right_re, right_im):
    real_part = contract(left_re, right_re) + contract(left_im, right_im)
    imag_part = contract(left_im, right_re) - contract(left_re, right_im)
    return (real_part, imag_part)


def local(state_real, state_imag, subsystem):
    local_bits = state_real.shape[0].bit_length() - 1
    count_rest = state_real.shape[0] // 8
    branches = regroup(local_bits)
    middle_place = jnp.clip(subsystem[1] - 1, 0, local_bits - 3)
    local_real = lax.switch(middle_place, branches, state_real)
    local_imag = lax.switch(middle_place, branches, state_imag)
    received_re, received_im = (
        lax.all_to_all(local_real, DEV, split_axis=1, concat_axis=0, tiled=True),
        lax.all_to_all(local_imag, DEV, split_axis=1, concat_axis=0, tiled=True),
    )
    full_width = received_re.shape[0]
    scale = 1.0 / count_rest
    left_re = lax.slice_in_dim(received_re, 0, full_width, axis=0)
    left_im = lax.slice_in_dim(received_im, 0, full_width, axis=0)
    real_part, imag_part = gram(left_re, left_im, received_re, received_im)
    own_rows = sum_by_chip(
        jnp.concatenate([real_part, imag_part], axis=1), ("dev_0", "dev_1", "dev_2"), "dev_3", 0
    )
    own_rows = own_rows * scale
    return (own_rows[:, :full_width], own_rows[:, full_width:])


def solution(mesh):
    finer = Mesh(mesh.devices.reshape(4, 4, 4, 2), ("dev_0", "dev_1", "dev_2", "dev_3"))
    return jax.shard_map(
        local,
        mesh=finer,
        in_specs=(P(DEV), P(DEV), P()),
        out_specs=(P(DEV, None), P(DEV, None)),
        check_vma=False,
    )
```

profile of v0, /device:TPU:0, one launch (start us, length us, event | category | flops | bytes accessed | tf_op | source)
XLA Modules:
  0.0 601.6 jit_solution(17882898776122956219)
XLA Ops:
  7.2 1.2 slice.9
  9.1 0.0 copy-start
  9.1 66.6 %conditional.2 = (f32[8,16384]{1,0:T(8,128)}) conditional(s32[]{:T(128)} %bitcast.30, f32[131072]{0:T(1024)} %param.33, f32[131072]{0:T(1024)} %param.33, f32[131072]{0:T(1024)} %param.33, f32[131072]{0:T(1024)} %param.33, f32[131072]{0:T(1024)} %param.33, f32[131072]{0:T(1024)} %param.33, ...), branch_computations={%region_0.1_spmd, %region_1.2_spmd, %region_2.3_spmd, %region_3.4_... | conditional | bytes 3145736 | solution.py:60
  21.2 35.6 %reshape.169 = f32[2,2,2,8192,2]{4,3,2,1,0:T(8,128)} reshape(f32[131072]{0:T(1024)} %param.13) | data formatting | bytes 1048576 | tf_op jit(solution)/shard_map/cond/branch_13_fun/reshape | solution.py:31
  56.8 17.6 %copy.32 = f32[2,2,2,2,8192]{4,3,2,1,0:T(2,128)S(1)} copy(f32[2,2,2,2,8192]{2,4,1,3,0:T(8,128)} %bitcast.149) | data formatting | bytes 1048576 | tf_op jit(solution)/shard_map/cond/branch_13_fun/transpose | solution.py:32
  74.4 1.1 copy.57
  75.6 0.0 copy-done
  75.7 11.7 %all-to-all-start = ((f32[8,128,128]{2,0,1:T(8,128)}), f32[8,128,128]{2,0,1:T(8,128)}, u32[]{:S(2)}, u32[]{:S(2)}) async-start(f32[8,128,128]{2,0,1:T(8,128)} %bitcast.31), calls=%async_computation | async-start | bytes 1048576 | tf_op jit(solution)/shard_map/all_to_all | solution.py:63
  87.4 65.8 %conditional.3 = (f32[8,16384]{1,0:T(8,128)}) conditional(s32[]{:T(128)} %bitcast.30, f32[131072]{0:T(1024)S(1)} %copy-done, f32[131072]{0:T(1024)S(1)} %copy-done, f32[131072]{0:T(1024)S(1)} %copy-done, f32[131072]{0:T(1024)S(1)} %copy-done, f32[131072]{0:T(1024)S(1)} %copy-done, f32[131072]{0:T(1024)S(1)} %copy-done, ...), branch_computations={%region_15.16_spmd, %region_16.17_spmd, %region_17.18_spmd, %regio... | conditional | bytes 3145736 | solution.py:61
  99.4 34.8 %reshape.199 = f32[2,2,2,8192,2]{4,3,2,1,0:T(8,128)} reshape(f32[131072]{0:T(1024)S(1)} %param.28) | data formatting | bytes 1048576 | tf_op jit(solution)/shard_map/cond/branch_13_fun/reshape | solution.py:31
  134.3 17.6 %copy.47 = f32[2,2,2,2,8192]{4,3,2,1,0:T(2,128)S(1)} copy(f32[2,2,2,2,8192]{2,4,1,3,0:T(8,128)} %bitcast.163) | data formatting | bytes 1048576 | tf_op jit(solution)/shard_map/cond/branch_13_fun/transpose | solution.py:32
  151.9 1.1 copy.64
  153.2 0.0 all-to-all-done
  153.2 9.7 %all-to-all-start.1 = ((f32[8,128,128]{2,0,1:T(8,128)}), f32[8,128,128]{2,0,1:T(8,128)S(1)}, u32[]{:S(2)}, u32[]{:S(2)}) async-start(f32[8,128,128]{2,0,1:T(8,128)} %bitcast.34), calls=%async_computation.1 | async-start | bytes 1048576 | tf_op jit(solution)/shard_map/all_to_all | solution.py:64
  162.9 0.0 reduce-scatter.3.cloned.1.call-start
  162.9 6.6 %fusion.3 = f32[1024,1024]{0,1:T(8,128)} fusion(f32[8,128,128]{2,0,1:T(8,128)} %all-to-all-done), kind=kOutput, calls=%fused_computation.8 | convolution fusion | flops 1610612736 | bytes 4718592 | tf_op jit(solution)/shard_map/dot_general | solution.py:40
  169.5 6.9 %all-to-all-done.1 = f32[8,128,128]{2,0,1:T(8,128)S(1)} async-done(((f32[8,128,128]{2,0,1:T(8,128)}), f32[8,128,128]{2,0,1:T(8,128)S(1)}, u32[]{:S(2)}, u32[]{:S(2)}) %all-to-all-start.1) | async-done | bytes 524320 | tf_op jit(solution)/shard_map/all_to_all | solution.py:64
  176.4 4.6 fusion.1
  181.0 4.7 convolution_subtract_fusion
  185.7 5.5 convolution_add_fusion
  191.2 4.1 pad_maximum_fusion
  195.2 9.2 %copy.49 = f32[1024,2048]{1,0:T(8,128)} copy(f32[1024,2048]{0,1:T(8,128)} %pad_maximum_fusion) | data formatting | bytes 16777216 | tf_op jit(solution)/shard_map/concatenate | solution.py:72
  204.4 7.7 %copy.50 = f32[2,64,8,2048]{3,2,1,0:T(8,128)} copy(f32[2,64,8,2048]{3,2,0,1:T(8,128)} %bitcast.166) | data formatting | bytes 16777216 | tf_op jit(solution)/shard_map/transpose | solution.py:19
  212.2 0.0 reduce-scatter.3.cloned.1.call-update
  212.2 0.0 reduce-scatter.5.cloned.1.call-start
  212.2 15.3 %reduce-scatter.3.cloned.1.call-done = f32[64,8,2048]{2,1,0:T(8,128)} async-done(((f32[128,8,2048]{2,1,0:T(8,128)}), f32[64,8,2048]{2,1,0:T(8,128)}) %reduce-scatter.3.cloned.1.call-update) | async-done | bytes 4194320 | tf_op jit(solution)/shard_map/reduce_scatter | solution.py:20
  227.5 0.0 reduce-scatter.5.cloned.1.call-update
  227.5 365.5 %reduce-scatter.5.cloned.1.call-done = f32[1,8,2048]{2,1,0:T(8,128)} async-done(((f32[64,8,2048]{2,1,0:T(8,128)}), f32[1,8,2048]{2,1,0:T(8,128)}) %reduce-scatter.5.cloned.1.call-update) | async-done | bytes 65552 | tf_op jit(solution)/shard_map/reduce_scatter | solution.py:21
  593.0 0.8 multiply_bitcast_fusion
  593.9 0.6 fusion.8
Async XLA Ops:
  9.1 66.6 %copy-start = (f32[131072]{0:T(1024)S(1)}, f32[131072]{0:T(1024)}, u32[]{:S(2)}) copy-start(f32[131072]{0:T(1024)} %param.34) | copy-start | bytes 1572868
  75.7 77.5 %all-to-all-start = ((f32[8,128,128]{2,0,1:T(8,128)}), f32[8,128,128]{2,0,1:T(8,128)}, u32[]{:S(2)}, u32[]{:S(2)}) async-start(f32[8,128,128]{2,0,1:T(8,128)} %bitcast.31), calls=%async_computation | async-start | bytes 1048576 | tf_op jit(solution)/shard_map/all_to_all | solution.py:63
  153.2 23.2 %all-to-all-start.1 = ((f32[8,128,128]{2,0,1:T(8,128)}), f32[8,128,128]{2,0,1:T(8,128)S(1)}, u32[]{:S(2)}, u32[]{:S(2)}) async-start(f32[8,128,128]{2,0,1:T(8,128)} %bitcast.34), calls=%async_computation.1 | async-start | bytes 1048576 | tf_op jit(solution)/shard_map/all_to_all | solution.py:64
  162.9 64.6 %reduce-scatter.3.cloned.1.call-start = ((), (), s32[]{:S(2)}) async-start(), calls=%async_computation.4 | async-start | bytes 12582912 | tf_op jit(solution)/shard_map/reduce_scatter | solution.py:20
  212.2 380.8 %reduce-scatter.5.cloned.1.call-start = ((), (), s32[]{:S(2)}) async-start(), calls=%async_computation.5 | async-start | bytes 4259840 | tf_op jit(solution)/shard_map/reduce_scatter | solution.py:21
Sparse Core Ops, SparseCore 0:
  212.3 15.1 reduce-scatter.2
  229.9 363.1 reduce-scatter.4
where the time goes:
time: 611 us; the launch traced here: 602 us
  waiting for transfers between devices  388 us (64%)
  local copies, waits for them, and re-layouts  127 us (21%)
  loops' own time  24.5 us (4%)
  starting transfers between devices  21.5 us (4%)
  matrix products  21.3 us (3%)
  between operations  15 us (2%)
    reduce_scatter x1, waiting for transfers between devices, sum_by_chip(): return lax.psum_scatter(blocks, chips, scatter_dimension=0, tiled=True)[0]  365 us
    reshape x2, local copies, waits for them, and re-layouts, make_branch(): shaped = flat.reshape(2, upper, 2, lower, 2)  70.4 us
    transpose x2, local copies, waits for them, and re-layouts, make_branch(): moved = jnp.transpose(shaped, (0, 2, 4, 1, 3))  35.2 us
    dot_general x4, matrix products, contract(): lax.dot_general(left, right, (((1,), (1,)), ((), ())), precision=lax.Prec...  21.3 us
    reduce_scatter x1, waiting for transfers between devices, sum_by_chip(): blocks = lax.psum_scatter(blocks, core, scatter_dimension=0, tiled=True)  15.3 us
    another operation x1, loops' own time, local(): local_real = lax.switch(middle_place, branches, state_real)  12.3 us
    another operation x1, loops' own time, local(): local_imag = lax.switch(middle_place, branches, state_imag)  12.2 us
  transfers between devices with their start and end apart: 4, of which 3 were waited for; matrix products, arithmetic and copies ran while one was open for 10% of the time, Pallas kernels for 0%

commit v1 on v0

v1 whole, which is shorter than its diff:
```python
import jax
import jax.numpy as jnp
from jax import lax
from jax.experimental import pallas as pl
from jax.experimental.pallas import tpu as pltpu
from jax.sharding import Mesh
from jax.sharding import PartitionSpec as P

DEV = ("yh", "yl", "zh", "zl", "xh", "xl", "c")
PEERS = ("yl", "zh", "zl", "xh", "xl")
LANES = 128
ROWS = 1024
PARTS = 8


def lane_source(middle, lane):
    low_top = lane >> 6
    rest6 = lane & 63
    plain = low_top | (rest6 << 1)
    m = jnp.clip(middle, 1, 6)
    rest5 = lane & 31
    below = rest5 & ((1 << (m - 1)) - 1)
    above = rest5 >> (m - 1)
    both = low_top | (below << 1) | (((lane >> 5) & 1) << m) | (above << (m + 1))
    return jnp.where(middle < 7, both, plain)


def sublane_source(middle, sub):
    m = jnp.clip(middle - 7, 0, 2)
    rest = sub & 3
    below = rest & ((1 << m) - 1)
    above = rest >> m
    return below | ((sub >> 2) << m) | (above << (m + 1))


def regroup_kernel(sub_ref, re_ref, im_ref, out_ref, buf, sems):
    middle = sub_ref[1]
    lane = lax.broadcasted_iota(jnp.int32, (8, LANES), 1)
    sub = lax.broadcasted_iota(jnp.int32, (8, LANES), 0)
    lane_index = lane_source(middle, lane)
    sub_index = sublane_source(middle, sub)
    low64 = lane < 64
    low32 = (lane & 32) == 0
    low4 = sub < 4

    def load(ref, tile):
        return ref[pl.ds(pl.multiple_of(tile * 8, 8), 8), :]

    def lanes(value):
        return jnp.take_along_axis(value, lane_index, axis=1)

    def swap64(a, b):
        return (
            jnp.where(low64, a, pltpu.roll(b, 64, 1)),
            jnp.where(low64, pltpu.roll(a, 64, 1), b),
        )

    def swap32(a, b):
        return (
            jnp.where(low32, a, pltpu.roll(b, 32, 1)),
            jnp.where(low32, pltpu.roll(a, 96, 1), b),
        )

    def swap_sub(a, b):
        return (
            jnp.where(low4, a, pltpu.roll(b, 4, 0)),
            jnp.where(low4, pltpu.roll(a, 4, 0), b),
        )

    def lane_case(ref, top, k4):
        base = top * 64 + k4 * 4
        a = [lanes(load(ref, base + r)) for r in range(4)]
        b00, b10 = swap64(a[0], a[2])
        b01, b11 = swap64(a[1], a[3])
        return (*swap32(b00, b01), *swap32(b10, b11))

    def sub_case(ref, top, k4):
        base = top * 64 + k4 * 4
        a = [jnp.take_along_axis(lanes(load(ref, base + r)), sub_index, axis=0) for r in range(4)]
        b00, b10 = swap64(a[0], a[2])
        b01, b11 = swap64(a[1], a[3])
        return (*swap_sub(b00, b01), *swap_sub(b10, b11))

    def tile_case(ref, top, k4):
        m = jnp.clip(middle - 10, 0, 5)
        out = []
        for bit in range(2):
            pair = []
            for r in range(2):
                rest = k4 * 2 + r
                below = rest & ((1 << m) - 1)
                above = rest >> m
                tile = top * 64 + (below | (bit << m) | (above << (m + 1)))
                pair.append(lanes(load(ref, tile)))
            out.append(swap64(*pair))
        return (out[0][0], out[1][0], out[0][1], out[1][1])

    def run(case):
        def step(k4, carry):
            for array, ref in enumerate((re_ref, im_ref)):
                for top in range(2):
                    tiles = case(ref, top, k4)
                    for which, tile in enumerate(tiles):
                        part = (which >> 1) + 2 * (which & 1) + 4 * top
                        row = (k4 >> 1) * 32 + array * 16 + (k4 & 1) * 8 + part
                        buf[pl.ds(row, 8, stride=256), :] = tile
            return carry

        lax.fori_loop(0, 16, step, 0)

    @pl.when(middle < 7)
    def _():
        run(lane_case)

    @pl.when((middle >= 7) & (middle < 10))
    def _():
        run(sub_case)

    @pl.when(middle >= 10)
    def _():
        run(tile_case)

    copies = [pltpu.make_async_copy(buf, out_ref.at[i], sems.at[i]) for i in range(2)]
    for copy in copies:
        copy.start()
    for copy in copies:
        copy.wait()


def regroup(subsystem, state_real, state_imag):
    half = 64 * 4 * PARTS
    return pl.pallas_call(
        regroup_kernel,
        out_shape=jax.ShapeDtypeStruct((2, half, LANES), jnp.float32),
        in_specs=[
            pl.BlockSpec(memory_space=pltpu.SMEM),
            pl.BlockSpec(memory_space=pltpu.VMEM),
            pl.BlockSpec(memory_space=pltpu.VMEM),
        ],
        out_specs=pl.BlockSpec(memory_space=pl.ANY),
        scratch_shapes=[pltpu.VMEM((half, LANES), jnp.float32), pltpu.SemaphoreType.DMA((2,))],
        name="regroup",
    )(subsystem, state_real.reshape(ROWS, LANES), state_imag.reshape(ROWS, LANES))


def split(value):
    high = value.astype(jnp.bfloat16)
    low = (value - high.astype(jnp.float32)).astype(jnp.bfloat16)
    return high, low


def gram_kernel(place_ref, left_own, left_other, right_own, right_other, out_ref, left):
    def rows(ref, array, index):
        return [
            ref[index + (slice(None), slice(array * 16 + u * 8, array * 16 + u * 8 + 8))].reshape(-1, LANES)
            for u in range(2)
        ]

    @pl.when(pl.program_id(0) == 0)
    def _():
        for half, ref in enumerate((left_own, left_other)):
            re = jnp.concatenate([v for v in rows(ref.at[0, :, 0], 0, ())], axis=1)
            im = jnp.concatenate([v for v in rows(ref.at[0, :, 0], 1, ())], axis=1)
            re_h, re_l = split(re)
            im_h, im_l = split(im)
            blocks = ((re_h, im_h), (re_h, im_h), (re_l, im_l), (im_h, -re_h), (im_h, -re_h), (im_l, -re_l))
            for j, (top, bottom) in enumerate(blocks):
                at = (half * 6 + j) * 256
                left[0:256, at : at + 256] = top
                left[256:512, at : at + 256] = bottom

    right = []
    for ref in (right_own, right_other):
        re_h, re_l = split(jnp.concatenate(rows(ref, 0, ()), axis=1))
        im_h, im_l = split(jnp.concatenate(rows(ref, 1, ()), axis=1))
        right += [re_h, re_l, re_h, im_h, im_l, im_h]
    result = lax.dot_general(
        left[...],
        jnp.concatenate(right, axis=1),
        (((1,), (1,)), ((), ())),
        preferred_element_type=jnp.float32,
    )
    out_ref[:, 0] = result[0:256].reshape(32, 8, 256)
    out_ref[:, 1] = result[256:512].reshape(32, 8, 256)


def gram(place, own, other):
    left_spec = pl.BlockSpec((1, 32, 1, 32, LANES), lambda i, place: (place[0], 0, place[1], 0, 0))
    right_spec = pl.BlockSpec((32, 32, LANES), lambda i, place: (i, 0, 0))
    own5, other5 = (v.reshape(2, 32, 2, 32, LANES) for v in (own, other))
    return pl.pallas_call(
        gram_kernel,
        out_shape=jax.ShapeDtypeStruct((32, 2, 8, 1024), jnp.float32),
        grid_spec=pltpu.PrefetchScalarGridSpec(
            num_scalar_prefetch=1,
            grid=(4,),
            in_specs=[left_spec, left_spec, right_spec, right_spec],
            out_specs=pl.BlockSpec((32, 2, 8, 256), lambda i, place: (0, 0, 0, i)),
            scratch_shapes=[pltpu.VMEM((512, 12 * 256), jnp.bfloat16)],
        ),
        compiler_params=pltpu.CompilerParams(dimension_semantics=("arbitrary",)),
        name="gram",
    )(place, own5, other5, own, other)


def local(state_real, state_imag, subsystem):
    sent = regroup(subsystem, state_real, state_imag).reshape(128, 32, LANES)
    own = lax.all_to_all(sent, DEV, 0, 0, tiled=True)
    other = lax.ppermute(own, "c", [(0, 1), (1, 0)])
    place = jnp.stack([lax.axis_index("yh"), lax.axis_index("c")]).astype(jnp.int32)
    partial = gram(place, own, other)
    received = lax.all_to_all(partial, PEERS, 0, 0, tiled=True)
    total = jnp.sum(received, axis=0) * (1.0 / 16384)
    return total[0], total[1]


def solution(mesh):
    finer = Mesh(mesh.devices.reshape((2,) * 7), DEV)
    return jax.shard_map(
        local,
        mesh=finer,
        in_specs=(P(DEV), P(DEV), P()),
        out_specs=(P(DEV, None), P(DEV, None)),
        check_vma=False,
    )
```

time: 611 us -> 93.7 us (0.15); the launches traced: 602 us -> 93.4 us
  waiting for transfers between devices: 388 us -> 3.58 us
  local copies, waits for them, and re-layouts: 127 us -> 0.63 us
  blocking collectives: 0 us -> 74.2 us
  loops' own time: 24.5 us -> 0 us
  starting transfers between devices: 21.5 us -> 0.01 us
  matrix products: 21.3 us -> 0 us
  between operations: 15 us -> 0.65 us
  Pallas kernels: 0 us -> 13.4 us
    reduce_scatter x2 -> x0, waiting for transfers between devices: 381 us -> none  [the longest x1 365 us: sum_by_chip(): return lax.psum_scatter(blocks, chips, scatter_dimension=0, tiled=True)[0]]
    all_to_all x0 -> x2, blocking collectives: none -> 74.2 us  [the longest x1 41.5 us: local(): own = lax.all_to_all(sent, DEV, 0, 0, tiled=True)]
    reshape x2 -> x0, local copies, waits for them, and re-layouts: 70.4 us -> none  [make_branch(): shaped = flat.reshape(2, upper, 2, lower, 2)]
    transpose x3 -> x0, local copies, waits for them, and re-layouts: 43 us -> none  [the longest x2 35.2 us: make_branch(): moved = jnp.transpose(shaped, (0, 2, 4, 1, 3))]
    another operation x2 -> x0, loops' own time: 24.5 us -> none  [the longest x1 12.3 us: local(): local_real = lax.switch(middle_place, branches, state_real)]
    all_to_all x2 -> x0, starting transfers between devices: 21.4 us -> none  [the longest x1 11.7 us: local(): lax.all_to_all(local_real, DEV, split_axis=1, concat_axis=0, tiled=True)]
    dot_general x4 -> x0, matrix products: 21.3 us -> none  [contract(): lax.dot_general(left, right, (((1,), (1,)), ((), ())), precision=lax.Prec...]
    pallas_call x0 -> x2, Pallas kernels: none -> 13.4 us  [the longest x1 8.01 us: gram(): pl.pallas_call(gram_kernel, out_shape=jax.ShapeDtypeStruct((32, 2, 8, 102...]
  transfers between devices with their start and end apart: 4 -> 1, of which waited for: 3 -> 1; matrix products, arithmetic and copies ran while one was open for 10% -> 1% of each run, Pallas kernels for 0% -> 0%
where the time goes in v1:
time: 93.7 us; the launch traced here: 93.4 us
  blocking collectives  74.2 us (79%)
  Pallas kernels  13.4 us (14%)
  waiting for transfers between devices  3.58 us (4%)
    all_to_all x1, blocking collectives, local(): own = lax.all_to_all(sent, DEV, 0, 0, tiled=True)  41.5 us
    all_to_all x1, blocking collectives, local(): received = lax.all_to_all(partial, PEERS, 0, 0, tiled=True)  32.7 us
    pallas_call x1, Pallas kernels, gram(): pl.pallas_call(gram_kernel, out_shape=jax.ShapeDtypeStruct((32, 2, 8, 102...  8.01 us
    pallas_call x1, Pallas kernels, regroup(): pl.pallas_call(regroup_kernel, out_shape=jax.ShapeDtypeStruct((2, half, L...  5.42 us
    ppermute x1, waiting for transfers between devices, local(): other = lax.ppermute(own, 'c', [(0, 1), (1, 0)])  3.58 us
  transfers between devices with their start and end apart: 1, of which 1 were waited for; matrix products, arithmetic and copies ran while one was open for 1% of the time, Pallas kernels for 0%

profile of v1, /device:TPU:0, one launch (start us, length us, event | category | flops | bytes accessed | tf_op | source)
XLA Modules:
  0.0 93.4 jit_solution(7691366555051327248)
XLA Ops:
  0.6 5.4 %regroup.1 = f32[2,2048,128]{2,1,0:T(8,128)} custom-call(s32[3]{0:T(128)} %sub_ref.1, f32[1024,128]{1,0:T(8,128)} %bitcast.13, f32[1024,128]{1,0:T(8,128)} %bitcast.14), custom_call_target="tpu_custom_call" | custom-call | tf_op jit(solution)/shard_map/regroup/pallas_call | solution.py:132
  6.1 41.5 %all_to_all.10.right_own = f32[128,32,128]{2,1,0:T(8,128)S(1)} all-to-all(f32[128,32,128]{2,1,0:T(8,128)} %bitcast.12), channel_id=1, replica_groups=mesh['yh'=2,'yl'=2,'zh'=2,'zl'=2,'xh'=2,'xl'=2,'c'=2] {'yh','yl','zh','z..., dimensions={0} | all-to-all | bytes 4194304 | tf_op jit(solution)/shard_map/all_to_all | solution.py:208
  47.6 0.0 copy-start
  47.6 0.0 collective-permute-start
  47.6 0.7 pad_add_fusion.place_ref
  48.3 3.6 %collective-permute-done.right_other = f32[128,32,128]{2,1,0:T(8,128)} collective-permute-done((f32[128,32,128]{2,1,0:T(8,128)S(1)}, f32[128,32,128]{2,1,0:T(8,128)}, u32[]{:S(2)}, u32[]{:S(2)}) %collective-permute-start) | collective-permute-done | bytes 2097184 | tf_op jit(solution)/shard_map/ppermute | solution.py:209
  51.9 0.0 copy-done
  51.9 8.0 %gram.1 = f32[32,2,8,1024]{3,2,1,0:T(8,128)} custom-call(s32[2]{0:T(128)} %pad_add_fusion.place_ref, f32[2,32,2,32,128]{4,3,2,1,0:T(8,128)} %bitcast.11, f32[2,32,2,32,128]{4,3,2,1,0:T(8,128)} %bitcast.6.left_other, f32[128,32,128]{2,1,0:T(8,128)} %copy-done, f32[128,32,128]{2,1,0:T(8,128)} %collective-permute-done.right_other), custom_call_target="tpu_custom_call" | custom-call | tf_op jit(solution)/shard_map/gram/pallas_call | solution.py:191
  59.9 32.7 %all_to_all.11 = f32[32,2,8,1024]{3,2,1,0:T(8,128)S(1)} all-to-all(f32[32,2,8,1024]{3,2,1,0:T(8,128)} %gram.1), channel_id=1, replica_groups=mesh['yh'=2,'yl'=2,'zh'=2,'zl'=2,'xh'=2,'xl'=2,'c'=2] {'yl','zh','zl','x..., dimensions={0} | all-to-all | bytes 4194304 | tf_op jit(solution)/shard_map/all_to_all | solution.py:212
  92.6 0.1 reduce_sum.9
  92.7 0.6 slice_bitcast_fusion
  (1 shorter events, 0.0 us)
Async XLA Ops:
  47.6 4.3 %copy-start = (f32[128,32,128]{2,1,0:T(8,128)}, f32[128,32,128]{2,1,0:T(8,128)S(1)}, u32[]{:S(2)}) copy-start(f32[128,32,128]{2,1,0:T(8,128)S(1)} %all_to_all.10.right_own) | copy-start | bytes 6291460
  47.6 4.3 %collective-permute-start = (f32[128,32,128]{2,1,0:T(8,128)S(1)}, f32[128,32,128]{2,1,0:T(8,128)}, u32[]{:S(2)}, u32[]{:S(2)}) collective-permute-start(f32[128,32,128]{2,1,0:T(8,128)S(1)} %all_to_all.10.right_own), channel_id=1, source_target_pairs={{0,1},{1,0},{2,3},{3,2},{4,5},{5,4},{6,7},{7,6},{8,9},{9,8},{10,11... | collective-permute-start | bytes 6291464 | tf_op jit(solution)/shard_map/ppermute | solution.py:209

commit v2 on v1

v2 whole, which is shorter than its diff:
```python
import jax
import jax.numpy as jnp
from jax import lax
from jax.experimental import pallas as pl
from jax.experimental.pallas import tpu as pltpu
from jax.sharding import Mesh
from jax.sharding import PartitionSpec as P

DEV = ("yh", "yl", "zh", "zl", "xh", "xl", "c")
PEERS = ("yl", "zh", "zl", "xh", "xl")
LANES = 128
ROWS = 1024
PARTS = 8
HALF = 64 * 4 * PARTS


def lane_source(middle, lane):
    low_top = lane >> 6
    rest6 = lane & 63
    plain = low_top | (rest6 << 1)
    m = jnp.clip(middle, 1, 6)
    rest5 = lane & 31
    below = rest5 & ((1 << (m - 1)) - 1)
    above = rest5 >> (m - 1)
    both = low_top | (below << 1) | (((lane >> 5) & 1) << m) | (above << (m + 1))
    return jnp.where(middle < 7, both, plain)


def sublane_source(middle, sub):
    m = jnp.clip(middle - 7, 0, 2)
    rest = sub & 3
    below = rest & ((1 << m) - 1)
    above = rest >> m
    return below | ((sub >> 2) << m) | (above << (m + 1))


def regroup_kernel(sub_ref, re_hbm, im_hbm, out_ref, re_ref, im_ref, tall, sems):
    copies = [
        pltpu.make_async_copy(src, dst, sems.at[i])
        for i, (src, dst) in enumerate(((re_hbm, re_ref), (im_hbm, im_ref)))
    ]
    for copy in copies:
        copy.start()
    middle = sub_ref[1]
    lane = lax.broadcasted_iota(jnp.int32, (8, LANES), 1)
    sub = lax.broadcasted_iota(jnp.int32, (8, LANES), 0)
    lane_index = lane_source(middle, lane)
    sub_index = sublane_source(middle, sub)
    low64 = lane < 64
    low32 = (lane & 32) == 0
    low4 = sub < 4

    def load(ref, tile):
        return ref[pl.ds(pl.multiple_of(tile * 8, 8), 8), :]

    def lanes(value):
        return jnp.take_along_axis(value, lane_index, axis=1)

    def swap64(a, b):
        return (
            jnp.where(low64, a, pltpu.roll(b, 64, 1)),
            jnp.where(low64, pltpu.roll(a, 64, 1), b),
        )

    def swap32(a, b):
        return (
            jnp.where(low32, a, pltpu.roll(b, 32, 1)),
            jnp.where(low32, pltpu.roll(a, 96, 1), b),
        )

    def swap_sub(a, b):
        return (
            jnp.where(low4, a, pltpu.roll(b, 4, 0)),
            jnp.where(low4, pltpu.roll(a, 4, 0), b),
        )

    def lane_case(ref, top, k4):
        base = top * 64 + k4 * 4
        a = [lanes(load(ref, base + r)) for r in range(4)]
        b00, b10 = swap64(a[0], a[2])
        b01, b11 = swap64(a[1], a[3])
        return (*swap32(b00, b01), *swap32(b10, b11))

    def sub_case(ref, top, k4):
        base = top * 64 + k4 * 4
        a = [jnp.take_along_axis(lanes(load(ref, base + r)), sub_index, axis=0) for r in range(4)]
        b00, b10 = swap64(a[0], a[2])
        b01, b11 = swap64(a[1], a[3])
        return (*swap_sub(b00, b01), *swap_sub(b10, b11))

    def tile_case(ref, top, k4):
        m = jnp.clip(middle - 10, 0, 5)
        out = []
        for bit in range(2):
            pair = []
            for r in range(2):
                rest = k4 * 2 + r
                below = rest & ((1 << m) - 1)
                above = rest >> m
                tile = top * 64 + (below | (bit << m) | (above << (m + 1)))
                pair.append(lanes(load(ref, tile)))
            out.append(swap64(*pair))
        return (out[0][0], out[1][0], out[0][1], out[1][1])

    def run(case, array, ref):
        def step(k4, carry):
            for top in range(2):
                for which, tile in enumerate(case(ref, top, k4)):
                    part = (which >> 1) + 2 * (which & 1) + 4 * top
                    tall[pl.ds((array * 16 + k4) * 72 + part * 9, 8), :] = tile
            return carry

        lax.fori_loop(0, 16, step, 0, unroll=4)

    for array, ref in enumerate((re_ref, im_ref)):
        copies[array].wait()

        @pl.when(middle < 7)
        def _():
            run(lane_case, array, ref)

        @pl.when((middle >= 7) & (middle < 10))
        def _():
            run(sub_case, array, ref)

        @pl.when(middle >= 10)
        def _():
            run(tile_case, array, ref)

    def finish(k4, carry):
        for array in range(2):
            for sub in range(8):
                tile = tall[pl.ds((array * 16 + k4) * 72 + sub, 8, stride=9), :]
                row = pl.multiple_of(sub * 256 + (k4 >> 1) * 32 + array * 16 + (k4 & 1) * 8, 8)
                out_ref[pl.ds(row, 8), :] = tile
                out_ref[pl.ds(row + HALF, 8), :] = tile
        return carry

    lax.fori_loop(0, 16, finish, 0, unroll=2)


def regroup(subsystem, state_real, state_imag):
    hbm = pl.BlockSpec(memory_space=pl.ANY)
    return pl.pallas_call(
        regroup_kernel,
        out_shape=pltpu.VMEM((2 * HALF, LANES), jnp.float32),
        in_specs=[pl.BlockSpec(memory_space=pltpu.SMEM), hbm, hbm],
        out_specs=pl.BlockSpec(memory_space=pltpu.VMEM),
        scratch_shapes=[
            pltpu.VMEM((ROWS, LANES), jnp.float32),
            pltpu.VMEM((ROWS, LANES), jnp.float32),
            pltpu.VMEM((2 * 16 * 72, LANES), jnp.float32),
            pltpu.SemaphoreType.DMA((2,)),
        ],
        compiler_params=pltpu.CompilerParams(vmem_limit_bytes=8 << 20),
        name="regroup",
    )(
        *(
            pltpu.with_memory_space_constraint(v, pltpu.HBM)
            for v in (subsystem, state_real.reshape(ROWS, LANES), state_imag.reshape(ROWS, LANES))
        )
    )


def split(value):
    high = value.astype(jnp.bfloat16)
    low = (value - high.astype(jnp.float32)).astype(jnp.bfloat16)
    return high, low


def gram_kernel(place_ref, given, *rest):
    added, out_ref = rest if len(rest) == 2 else (None, rest[0])

    def columns(ref, array):
        return split(
            jnp.concatenate(
                [ref[:, array * 16 + u * 8 : array * 16 + u * 8 + 8].reshape(-1, LANES) for u in range(2)],
                axis=1,
            )
        )

    mine = given.at[place_ref[0], :, place_ref[1]]
    re_h, re_l = columns(mine, 0)
    im_h, im_l = columns(mine, 1)
    top = [re_h, re_h, re_l, im_h, im_h, im_l]
    bottom = [im_h, im_h, im_l, -re_h, -re_h, -re_l]
    left = jnp.concatenate([jnp.concatenate(top, axis=1), jnp.concatenate(bottom, axis=1)], axis=0)
    flat = given.reshape(128, 32, LANES)
    for n in range(4):
        cut = flat.at[pl.ds(n * 32, 32)]
        re_h, re_l = columns(cut, 0)
        im_h, im_l = columns(cut, 1)
        result = lax.dot_general(
            left,
            jnp.concatenate([re_h, re_l, re_h, im_h, im_l, im_h], axis=1),
            (((1,), (1,)), ((), ())),
            preferred_element_type=jnp.float32,
        )
        at = slice(n * 256, n * 256 + 256)
        for array in range(2):
            part = result[array * 256 : array * 256 + 256].reshape(32, 8, 256)
            out_ref[:, array, :, at] = part if added is None else (part + added[:, array, :, at]) * (1.0 / 16384)


def gram(place, given, added=None):
    vmem = pl.BlockSpec(memory_space=pltpu.VMEM)
    extra = () if added is None else (added,)
    flops = 2 * 512 * 1024 * 6 * 256
    return pl.pallas_call(
        gram_kernel,
        out_shape=pltpu.VMEM((32, 2, 8, 1024), jnp.float32),
        in_specs=[pl.BlockSpec(memory_space=pltpu.SMEM), vmem, *(vmem for _ in extra)],
        out_specs=vmem,
        input_output_aliases={2: 0} if extra else {},
        compiler_params=pltpu.CompilerParams(vmem_limit_bytes=24 << 20),
        cost_estimate=pl.CostEstimate(flops=flops, transcendentals=0, bytes_accessed=4 << 20),
        name=f"gram{len(extra)}",
    )(place, given.reshape(2, 32, 2, 32, LANES), *extra)


def local(state_real, state_imag, subsystem):
    sent = regroup(subsystem, state_real, state_imag).reshape(128, 32, LANES)
    own = lax.all_to_all(sent, DEV, 0, 0, tiled=True)
    other = lax.ppermute(own, "c", [(0, 1), (1, 0)])
    place = jnp.stack([lax.axis_index("yh"), lax.axis_index("c")]).astype(jnp.int32)
    partial = gram(place, other, gram(place, own))
    received = lax.all_to_all(partial, PEERS, 0, 0, tiled=True)
    return jnp.sum(received[:, 0], axis=0), jnp.sum(received[:, 1], axis=0)


def solution(mesh):
    finer = Mesh(mesh.devices.reshape((2,) * 7), DEV)
    return jax.shard_map(
        local,
        mesh=finer,
        in_specs=(P(DEV), P(DEV), P()),
        out_specs=(P(DEV, None), P(DEV, None)),
        check_vma=False,
    )
```

time: 93.7 us -> 85.4 us (0.911)
  Pallas kernels: 13.4 us -> 9.61 us
  waiting for transfers between devices: 3.58 us -> 0.86 us
  blocking collectives: 74.2 us -> 73.2 us
    pallas_call x2 -> x3, Pallas kernels: 13.4 us -> 9.61 us  [the longest x2 6.14 us: gram(): pl.pallas_call(gram_kernel, out_shape=pltpu.VMEM((32, 2, 8, 1024), jnp.fl...]
    ppermute x1, waiting for transfers between devices: 3.58 us -> 0.86 us  [local(): other = lax.ppermute(own, 'c', [(0, 1), (1, 0)])]
  transfers between devices with their start and end apart: 1 -> 1, of which waited for: 1 -> 1; matrix products, arithmetic and copies ran while one was open for 1% -> 0% of each run, Pallas kernels for 0% -> 4%
where the time goes in v2:
time: 85.4 us; the launch traced here: 85.1 us
  blocking collectives  73.2 us (86%)
  Pallas kernels  9.61 us (11%)
  waiting for transfers between devices  0.86 us (1%)
    all_to_all x1, blocking collectives, local(): own = lax.all_to_all(sent, DEV, 0, 0, tiled=True)  41.4 us
    all_to_all x1, blocking collectives, local(): received = lax.all_to_all(partial, PEERS, 0, 0, tiled=True)  31.7 us
    pallas_call x2, Pallas kernels, gram(): pl.pallas_call(gram_kernel, out_shape=pltpu.VMEM((32, 2, 8, 1024), jnp.fl...  6.14 us
    pallas_call x1, Pallas kernels, regroup(): pl.pallas_call(regroup_kernel, out_shape=pltpu.VMEM((2 * HALF, LANES), jn...  3.47 us
  transfers between devices with their start and end apart: 1, of which 1 were waited for; matrix products, arithmetic and copies ran while one was open for 0% of the time, Pallas kernels for 4%

profile of v2, /device:TPU:0, one launch (start us, length us, event | category | flops | bytes accessed | tf_op | source)
XLA Modules:
  0.0 85.1 jit_solution(8467630763502016472)
XLA Ops:
  0.6 3.5 %regroup.1 = f32[4096,128]{1,0:T(8,128)S(1)} custom-call(s32[3]{0:T(128)} %sub_ref.1, f32[1024,128]{1,0:T(8,128)} %bitcast.9, f32[1024,128]{1,0:T(8,128)} %bitcast.10), custom_call_target="tpu_custom_call" | custom-call | tf_op jit(solution)/shard_map/regroup/pallas_call | solution.py:144
  4.1 41.4 %all_to_all.10 = f32[128,32,128]{2,1,0:T(8,128)} all-to-all(f32[128,32,128]{2,1,0:T(8,128)S(1)} %bitcast.7), channel_id=1, replica_groups=mesh['yh'=2,'yl'=2,'zh'=2,'zl'=2,'xh'=2,'xl'=2,'c'=2] {'yh','yl','zh','z..., dimensions={0} | all-to-all | bytes 4194304 | tf_op jit(solution)/shard_map/all_to_all | solution.py:223
  45.5 0.0 collective-permute-start
  45.6 0.1 pad_add_fusion.place_ref
  45.6 3.4 %gram0.1.rest_0_ = f32[32,2,8,1024]{3,2,1,0:T(8,128)S(1)} custom-call(s32[2]{0:T(128)S(1)} %pad_add_fusion.place_ref, f32[2,32,2,32,128]{4,3,2,1,0:T(8,128)} %bitcast.6.given), custom_call_target="tpu_custom_call" | custom-call | flops 1610612736 | bytes 4194304 | tf_op jit(solution)/shard_map/gram0/pallas_call | solution.py:209
  49.1 0.9 %collective-permute-done = f32[128,32,128]{2,1,0:T(8,128)S(1)} collective-permute-done((f32[128,32,128]{2,1,0:T(8,128)}, f32[128,32,128]{2,1,0:T(8,128)S(1)}, u32[]{:S(2)}, u32[]{:S(2)}) %collective-permute-start) | collective-permute-done | bytes 2097184 | tf_op jit(solution)/shard_map/ppermute | solution.py:224
  49.9 2.7 %gram1.1 = f32[32,2,8,1024]{3,2,1,0:T(8,128)S(1)} custom-call(s32[2]{0:T(128)S(1)} %pad_add_fusion.place_ref, f32[2,32,2,32,128]{4,3,2,1,0:T(8,128)S(1)} %bitcast.8, f32[32,2,8,1024]{3,2,1,0:T(8,128)S(1)} %gram0.1.rest_0_), custom_call_target="tpu_custom_call", output_to_operand_aliasing={{}: (2, {})} | custom-call | flops 1610612736 | bytes 4194304 | tf_op jit(solution)/shard_map/gram1/pallas_call | solution.py:209
  52.6 31.7 %all_to_all.11 = f32[32,2,8,1024]{3,2,1,0:T(8,128)S(1)} all-to-all(f32[32,2,8,1024]{3,2,1,0:T(8,128)S(1)} %gram1.1), channel_id=1, replica_groups=mesh['yh'=2,'yl'=2,'zh'=2,'zl'=2,'xh'=2,'xl'=2,'c'=2] {'yl','zh','zl','x..., dimensions={0} | all-to-all | bytes 4194304 | tf_op jit(solution)/shard_map/all_to_all | solution.py:227
  84.4 0.7 slice_reduce_fusion
Async XLA Ops:
  45.5 4.4 %collective-permute-start = (f32[128,32,128]{2,1,0:T(8,128)}, f32[128,32,128]{2,1,0:T(8,128)S(1)}, u32[]{:S(2)}, u32[]{:S(2)}) collective-permute-start(f32[128,32,128]{2,1,0:T(8,128)} %all_to_all.10), channel_id=1, source_target_pairs={{0,1},{1,0},{2,3},{3,2},{4,5},{5,4},{6,7},{7,6},{8,9},{9,8},{10,11... | collective-permute-start | bytes 6291464 | tf_op jit(solution)/shard_map/ppermute | solution.py:224

commit v3 on v2

--- a/solution.py
+++ b/solution.py
@@ -11,18 +11,19 @@
 LANES = 128
 ROWS = 1024
 PARTS = 8
+TERMS = 2
 HALF = 64 * 4 * PARTS
 
 
-def lane_source(middle, lane):
-    low_top = lane >> 6
-    rest6 = lane & 63
-    plain = low_top | (rest6 << 1)
+def mixing_source(middle, column):
+    quad, lane = column >> 7, column & 127
+    low, other = quad >> 1, quad & 1
     m = jnp.clip(middle, 1, 6)
     rest5 = lane & 31
     below = rest5 & ((1 << (m - 1)) - 1)
     above = rest5 >> (m - 1)
-    both = low_top | (below << 1) | (((lane >> 5) & 1) << m) | (above << (m + 1))
+    both = ((lane >> 5) << 7) | low | (below << 1) | (other << m) | (above << (m + 1))
+    plain = (other << 8) | ((lane >> 6) << 7) | low | ((lane & 63) << 1)
     return jnp.where(middle < 7, both, plain)
 
 
@@ -34,7 +35,7 @@
     return below | ((sub >> 2) << m) | (above << (m + 1))
 
 
-def regroup_kernel(sub_ref, re_hbm, im_hbm, out_ref, re_ref, im_ref, tall, sems):
+def regroup_kernel(sub_ref, re_hbm, im_hbm, out_ref, re_ref, im_ref, terms, tall, sems):
     copies = [
         pltpu.make_async_copy(src, dst, sems.at[i])
         for i, (src, dst) in enumerate(((re_hbm, re_ref), (im_hbm, im_ref)))
@@ -42,101 +43,76 @@
     for copy in copies:
         copy.start()
     middle = sub_ref[1]
-    lane = lax.broadcasted_iota(jnp.int32, (8, LANES), 1)
-    sub = lax.broadcasted_iota(jnp.int32, (8, LANES), 0)
-    lane_index = lane_source(middle, lane)
-    sub_index = sublane_source(middle, sub)
-    low64 = lane < 64
-    low32 = (lane & 32) == 0
-    low4 = sub < 4
-
-    def load(ref, tile):
+    source = mixing_source(middle, lax.broadcasted_iota(jnp.int32, (16, 512), 1))
+    source = source - lax.broadcasted_iota(jnp.int32, (16, 512), 0)
+    mixing = jnp.concatenate(
+        [jnp.where(source == 16 * i, 1.0, 0.0).astype(jnp.bfloat16) for i in range(32)], axis=0
+    )
+    place = jnp.where(middle >= 10, middle - 10, 1)
+
+    def load(ref, top, k4, r):
+        rest = k4 * 2 + (r & 1)
+        below = rest & ((1 << place) - 1)
+        tile = top * 64 + (below | ((r >> 1) << place) | ((rest >> place) << (place + 1)))
         return ref[pl.ds(pl.multiple_of(tile * 8, 8), 8), :]
-
-    def lanes(value):
-        return jnp.take_along_axis(value, lane_index, axis=1)
-
-    def swap64(a, b):
-        return (
-            jnp.where(low64, a, pltpu.roll(b, 64, 1)),
-            jnp.where(low64, pltpu.roll(a, 64, 1), b),
-        )
-
-    def swap32(a, b):
-        return (
-            jnp.where(low32, a, pltpu.roll(b, 32, 1)),
-            jnp.where(low32, pltpu.roll(a, 96, 1), b),
-        )
-
-    def swap_sub(a, b):
-        return (
-            jnp.where(low4, a, pltpu.roll(b, 4, 0)),
-            jnp.where(low4, pltpu.roll(a, 4, 0), b),
-        )
-
-    def lane_case(ref, top, k4):
-        base = top * 64 + k4 * 4
-        a = [lanes(load(ref, base + r)) for r in range(4)]
-        b00, b10 = swap64(a[0], a[2])
-        b01, b11 = swap64(a[1], a[3])
-        return (*swap32(b00, b01), *swap32(b10, b11))
-
-    def sub_case(ref, top, k4):
-        base = top * 64 + k4 * 4
-        a = [jnp.take_along_axis(lanes(load(ref, base + r)), sub_index, axis=0) for r in range(4)]
-        b00, b10 = swap64(a[0], a[2])
-        b01, b11 = swap64(a[1], a[3])
-        return (*swap_sub(b00, b01), *swap_sub(b10, b11))
-
-    def tile_case(ref, top, k4):
-        m = jnp.clip(middle - 10, 0, 5)
-        out = []
-        for bit in range(2):
-            pair = []
-            for r in range(2):
-                rest = k4 * 2 + r
-                below = rest & ((1 << m) - 1)
-                above = rest >> m
-                tile = top * 64 + (below | (bit << m) | (above << (m + 1)))
-                pair.append(lanes(load(ref, tile)))
-            out.append(swap64(*pair))
-        return (out[0][0], out[1][0], out[0][1], out[1][1])
-
-    def run(case, array, ref):
-        def step(k4, carry):
-            for top in range(2):
-                for which, tile in enumerate(case(ref, top, k4)):
-                    part = (which >> 1) + 2 * (which & 1) + 4 * top
-                    tall[pl.ds((array * 16 + k4) * 72 + part * 9, 8), :] = tile
-            return carry
-
-        lax.fori_loop(0, 16, step, 0, unroll=4)
 
     for array, ref in enumerate((re_ref, im_ref)):
         copies[array].wait()
 
-        @pl.when(middle < 7)
-        def _():
-            run(lane_case, array, ref)
-
-        @pl.when((middle >= 7) & (middle < 10))
-        def _():
-            run(sub_case, array, ref)
-
-        @pl.when(middle >= 10)
-        def _():
-            run(tile_case, array, ref)
-
-    def finish(k4, carry):
-        for array in range(2):
+        def fill(i, carry):
+            for top in range(2):
+                row = pl.multiple_of(top * 128 + i * 16, 16)
+                for r in range(4):
+                    value = jnp.concatenate([load(ref, top, 2 * i + j, r) for j in range(2)], axis=0)
+                    for t in range(TERMS):
+                        term = value.astype(jnp.bfloat16)
+                        terms[pl.ds(array * 256 + row, 16), t * 512 + r * 128 : t * 512 + r * 128 + 128] = term
+                        value = value - term.astype(jnp.float32)
+            return carry
+
+        lax.fori_loop(0, 8, fill, 0, unroll=8)
+
+    mixed = lax.dot_general(
+        terms[...],
+        jnp.concatenate([mixing] * TERMS, axis=0),
+        (((1,), (0,)), ((), ())),
+        preferred_element_type=jnp.float32,
+    )
+    for array in range(2):
+        for top in range(2):
+            for k4 in range(16):
+                row = array * 256 + top * 128 + k4 * 8
+                for quad in range(4):
+                    part = (quad >> 1) + 2 * (quad & 1) + 4 * top
+                    at = (array * 16 + k4) * 72 + part * 9
+                    tall[at : at + 8, :] = mixed[row : row + 8, quad * 128 : quad * 128 + 128]
+
+    @pl.when((middle >= 7) & (middle < 10))
+    def _():
+        sub = lax.broadcasted_iota(jnp.int32, (8, LANES), 0)
+        sub_index = sublane_source(middle, sub)
+        low4 = sub < 4
+
+        def swap(group, carry):
+            for part in (0, 1, 4, 5):
+                at = [pl.ds(group * 72 + p * 9, 8) for p in (part, part + 2)]
+                a, b = (jnp.take_along_axis(tall[rows, :], sub_index, axis=0) for rows in at)
+                tall[at[0], :] = jnp.where(low4, a, pltpu.roll(b, 4, 0))
+                tall[at[1], :] = jnp.where(low4, pltpu.roll(a, 4, 0), b)
+            return carry
+
+        lax.fori_loop(0, 32, swap, 0, unroll=8)
+
+    for array in range(2):
+        def finish(k4, carry):
             for sub in range(8):
                 tile = tall[pl.ds((array * 16 + k4) * 72 + sub, 8, stride=9), :]
                 row = pl.multiple_of(sub * 256 + (k4 >> 1) * 32 + array * 16 + (k4 & 1) * 8, 8)
                 out_ref[pl.ds(row, 8), :] = tile
                 out_ref[pl.ds(row + HALF, 8), :] = tile
-        return carry
-
-    lax.fori_loop(0, 16, finish, 0, unroll=2)
+            return carry
+
+        lax.fori_loop(0, 16, finish, 0, unroll=16)
 
 
 def regroup(subsystem, state_real, state_imag):
@@ -149,10 +125,11 @@
         scratch_shapes=[
             pltpu.VMEM((ROWS, LANES), jnp.float32),
             pltpu.VMEM((ROWS, LANES), jnp.float32),
+            pltpu.VMEM((512, TERMS * 512), jnp.bfloat16),
             pltpu.VMEM((2 * 16 * 72, LANES), jnp.float32),
             pltpu.SemaphoreType.DMA((2,)),
         ],
-        compiler_params=pltpu.CompilerParams(vmem_limit_bytes=8 << 20),
+        compiler_params=pltpu.CompilerParams(vmem_limit_bytes=12 << 20),
         name="regroup",
     )(
         *(

time: 85.4 us -> 84.7 us (level)
  no operation moved by 1% of the time
where the time goes in v3:
time: 84.7 us; the launch traced here: 84.5 us
  blocking collectives  73.2 us (86%)
  Pallas kernels  8.94 us (11%)
  waiting for transfers between devices  0.86 us (1%)
    all_to_all x1, blocking collectives, local(): own = lax.all_to_all(sent, DEV, 0, 0, tiled=True)  41.4 us
    all_to_all x1, blocking collectives, local(): received = lax.all_to_all(partial, PEERS, 0, 0, tiled=True)  31.7 us
    pallas_call x2, Pallas kernels, gram(): pl.pallas_call(gram_kernel, out_shape=pltpu.VMEM((32, 2, 8, 1024), jnp.fl...  6.14 us
    pallas_call x1, Pallas kernels, regroup(): pl.pallas_call(regroup_kernel, out_shape=pltpu.VMEM((2 * HALF, LANES), jn...  2.8 us
  transfers between devices with their start and end apart: 1, of which 1 were waited for; matrix products, arithmetic and copies ran while one was open for 0% of the time, Pallas kernels for 4%

profile of v3, /device:TPU:0, one launch (start us, length us, event | category | flops | bytes accessed | tf_op | source)
XLA Modules:
  0.0 84.5 jit_solution(5434667698109810789)
XLA Ops:
  0.6 2.8 %regroup.1 = f32[4096,128]{1,0:T(8,128)S(1)} custom-call(s32[3]{0:T(128)} %sub_ref.1, f32[1024,128]{1,0:T(8,128)} %bitcast.9, f32[1024,128]{1,0:T(8,128)} %bitcast.10), custom_call_target="tpu_custom_call" | custom-call | tf_op jit(solution)/shard_map/regroup/pallas_call | solution.py:120
  3.4 41.4 %all_to_all.10 = f32[128,32,128]{2,1,0:T(8,128)} all-to-all(f32[128,32,128]{2,1,0:T(8,128)S(1)} %bitcast.7), channel_id=1, replica_groups=mesh['yh'=2,'yl'=2,'zh'=2,'zl'=2,'xh'=2,'xl'=2,'c'=2] {'yh','yl','zh','z..., dimensions={0} | all-to-all | bytes 4194304 | tf_op jit(solution)/shard_map/all_to_all | solution.py:200
  44.9 0.0 collective-permute-start
  44.9 0.1 pad_add_fusion.place_ref
  45.0 3.4 %gram0.1.rest_0_ = f32[32,2,8,1024]{3,2,1,0:T(8,128)S(1)} custom-call(s32[2]{0:T(128)S(1)} %pad_add_fusion.place_ref, f32[2,32,2,32,128]{4,3,2,1,0:T(8,128)} %bitcast.6.given), custom_call_target="tpu_custom_call" | custom-call | flops 1610612736 | bytes 4194304 | tf_op jit(solution)/shard_map/gram0/pallas_call | solution.py:186
  48.4 0.9 %collective-permute-done = f32[128,32,128]{2,1,0:T(8,128)S(1)} collective-permute-done((f32[128,32,128]{2,1,0:T(8,128)}, f32[128,32,128]{2,1,0:T(8,128)S(1)}, u32[]{:S(2)}, u32[]{:S(2)}) %collective-permute-start) | collective-permute-done | bytes 2097184 | tf_op jit(solution)/shard_map/ppermute | solution.py:201
  49.3 2.7 %gram1.1 = f32[32,2,8,1024]{3,2,1,0:T(8,128)S(1)} custom-call(s32[2]{0:T(128)S(1)} %pad_add_fusion.place_ref, f32[2,32,2,32,128]{4,3,2,1,0:T(8,128)S(1)} %bitcast.8, f32[32,2,8,1024]{3,2,1,0:T(8,128)S(1)} %gram0.1.rest_0_), custom_call_target="tpu_custom_call", output_to_operand_aliasing={{}: (2, {})} | custom-call | flops 1610612736 | bytes 4194304 | tf_op jit(solution)/shard_map/gram1/pallas_call | solution.py:186
  52.0 31.7 %all_to_all.11 = f32[32,2,8,1024]{3,2,1,0:T(8,128)S(1)} all-to-all(f32[32,2,8,1024]{3,2,1,0:T(8,128)S(1)} %gram1.1), channel_id=1, replica_groups=mesh['yh'=2,'yl'=2,'zh'=2,'zl'=2,'xh'=2,'xl'=2,'c'=2] {'yl','zh','zl','x..., dimensions={0} | all-to-all | bytes 4194304 | tf_op jit(solution)/shard_map/all_to_all | solution.py:204
  83.7 0.7 slice_reduce_fusion
Async XLA Ops:
  44.9 4.4 %collective-permute-start = (f32[128,32,128]{2,1,0:T(8,128)}, f32[128,32,128]{2,1,0:T(8,128)S(1)}, u32[]{:S(2)}, u32[]{:S(2)}) collective-permute-start(f32[128,32,128]{2,1,0:T(8,128)} %all_to_all.10), channel_id=1, source_target_pairs={{0,1},{1,0},{2,3},{3,2},{4,5},{5,4},{6,7},{7,6},{8,9},{9,8},{10,11... | collective-permute-start | bytes 6291464 | tf_op jit(solution)/shard_map/ppermute | solution.py:201
